TPU v7x, 512 devices: a whole 4x8x8 slice. The times are simulated.
512 devices in a mesh: elem: 32 (over z, x), lev: 16 (over y, core).
Axes of the slice: x: 4, y: 8, z: 8, core: 2. Of those that a mesh axis runs over, the one named last changes fastest.
Arguments:
- cloud_state: float32 [4096, 8, 4096], P(('elem', 'lev')), may hold values from -6 to 6
- substeps: int32 [4096], P('elem'), may hold values from 4 to 16
- element_links: int32 [1024, 4], P('elem'), may hold values from 0 to 1023, as said below
- host_state: float32 [4, 64, 16384], P(None, 'lev', 'elem'), may hold values from -6 to 6
- wind_field: float32 [2, 64, 16384], P(None, 'lev', 'elem'), may hold values from -3 to 3
- node_mass: float32 [16384], P('elem'), may hold values from 0.25 to 4
- field_coupling: float32 [8, 8], replicated, may hold values from -2 to 2
- force_map: float32 [8, 4], replicated, may hold values from -3 to 3
- feedback_map: float32 [4, 8], replicated, may hold values from -5 to 5
Outputs:
- cloud_new: float32 [4096, 8, 4096], P(('elem', 'lev'))
- host_new: float32 [4, 64, 16384], P(None, 'lev', 'elem')
Inputs may be any that keep to these rules, and one draw needn't show every extreme that they name: `element_links`: the 1024 elements form a doubly periodic grid of 16 rows in which each index of elem holds two neighbouring grid columns, all rows, in some order; element e lies on index e // 32 of elem. Entries 0 to 3 of row e give the global index of the element to the left, right, below and above element e. An element's right edge meets its right neighbour's left edge node for node (same j), its upper edge its upper neighbour's lower edge (same i). The left neighbour lies on the same index of elem or the one before it (cyclically), the right one on the same or the one after it, the lower and upper ones on the same index.
All inputs are finite; a program needn't handle non-finite values.
Results may differ from a plain program's by a relative error of at most 0.0003.
Values sent between devices are 32-bit elements; how exact they have to be, the bound alone decides.
No kernel may reach another device: no remote copies, remote signals or barrier semaphores. Data moves between devices by JAX's collectives and lax.ppermute only.
A program may use at most 64 MiB of HBM per device.

v0:
```python
import jax
import jax.numpy as jnp
import numpy as np
from jax import lax
from jax.sharding import PartitionSpec as P

CRM_X = 64
lateral_mix = 0.2
vertical_mix = 0.2
cloud_step = 0.1
host_step = 0.1
host_mix = 0.2
highest = lax.Precision.HIGHEST


def padded_2(cells, sides, width, closed):
    for axis, dim in sides:
        count = lax.axis_size(axis)
        ends = count if closed else count - 1
        head = lax.slice_in_dim(cells, 0, width, axis=dim)
        tail = lax.slice_in_dim(cells, cells.shape[dim] - width, cells.shape[dim], axis=dim)
        cells = jnp.concatenate(
            [
                lax.ppermute(tail, axis, [(i, (i + 1) % count) for i in range(ends)]),
                cells,
                lax.ppermute(head, axis, [((i + 1) % count, i) for i in range(ends)]),
            ],
            axis=dim,
        )
    return cells


def gll_derivative():
    points = np.array([-1.0, -1.0 / np.sqrt(5.0), 1.0 / np.sqrt(5.0), 1.0])
    weights = np.array(
        [
            1.0 / np.prod([points[index] - points[other] for other in range(4) if other != index])
            for index in range(4)
        ]
    )
    matrix = np.zeros((4, 4))
    for target in range(4):
        for source in range(4):
            if target != source:
                matrix[target, source] = (
                    weights[source] / weights[target] / (points[target] - points[source])
                )
        matrix[target, target] = -np.sum(matrix[target])
    return matrix


def advance_clouds(cloud, driving, counts, coupling):
    n_rows, n_fields, n_cells = cloud.shape
    cell_width = CRM_X
    n_levels = n_cells // cell_width
    spread = jnp.repeat(driving, cell_width, axis=2)

    def one_step(stepno, current):
        extended = jnp.pad(current, ((0, 0), (0, 0), (cell_width, cell_width)))
        upper_cells = extended[:, :, 2 * cell_width :]
        lower_cells = extended[:, :, : -2 * cell_width]
        shaped = current.reshape(n_rows, n_fields, n_levels, cell_width)
        eastward = jnp.roll(shaped, -1, axis=3).reshape(current.shape)
        westward = jnp.roll(shaped, 1, axis=3).reshape(current.shape)
        reaction = jnp.tanh(jnp.einsum("gf,nfc->ngc", coupling, current, precision=highest))
        update = (
            current
            + (
                lateral_mix * (eastward + westward - 2.0 * current)
                + vertical_mix * (upper_cells + lower_cells - 2.0 * current)
            )
            + cloud_step * (reaction + spread)
        )
        return jnp.where((stepno < counts)[:, None, None], update, current)

    return lax.fori_loop(0, jnp.max(counts), one_step, cloud)


def edge_tables(element_links, n_nodes):
    elem_dev = n_nodes // 16
    quarter = 4 * elem_dev
    my_index = lax.axis_index("elem")
    node_ids = jnp.arange(n_nodes, dtype=jnp.int32)
    elem_of = node_ids // 16
    row_of = node_ids // 4 % 4
    col_of = node_ids % 4
    edge_ids = jnp.arange(2 * quarter, dtype=jnp.int32)
    inner = edge_ids % quarter
    edge_node = inner // 4 * 16 + inner % 4 * 4 + jnp.where(edge_ids < quarter, 0, 3)
    picker = (node_ids[:, None] == edge_node[None, :]).astype(jnp.float32)
    left_ids = element_links[:, 0][elem_of]
    right_ids = element_links[:, 1][elem_of]
    left_base = jnp.where(left_ids // elem_dev == my_index, 2 * quarter, 0)
    right_base = jnp.where(right_ids // elem_dev == my_index, 2 * quarter, 4 * quarter)
    left_source = left_base + quarter + left_ids % elem_dev * 4 + row_of
    right_source = right_base + right_ids % elem_dev * 4 + row_of
    side_source = jnp.where(col_of == 0, left_source, jnp.where(col_of == 3, right_source, -1))
    sideways = (jnp.arange(6 * quarter, dtype=jnp.int32)[:, None] == side_source[None, :]).astype(
        jnp.float32
    )
    lower_ids = element_links[:, 2][elem_of] % elem_dev
    upper_ids = element_links[:, 3][elem_of] % elem_dev
    lower_source = lower_ids * 16 + 12 + col_of
    upper_source = upper_ids * 16 + col_of
    vert_source = jnp.where(row_of == 0, lower_source, jnp.where(row_of == 3, upper_source, -1))
    vertical = (node_ids[:, None] == vert_source[None, :]).astype(jnp.float32)
    return (picker, sideways, vertical)


def edge_sum(quantity, tables):
    picker, sideways, vertical = tables
    lead, levels, n_nodes = quantity.shape
    flat = quantity.reshape(lead * levels, n_nodes)
    edges = jnp.dot(flat, picker, precision=highest).reshape(lead, levels, picker.shape[1])
    with_peers = padded_2(edges, (("elem", 2),), picker.shape[1], True)
    first = flat + jnp.dot(
        with_peers.reshape(lead * levels, sideways.shape[0]), sideways, precision=highest
    )
    second = first + jnp.dot(first, vertical, precision=highest)
    return second.reshape(lead, levels, n_nodes)


def shards(
    cloud_state,
    substeps,
    element_links,
    host_state,
    wind_field,
    node_mass,
    field_coupling,
    force_map,
    feedback_map,
):
    own_rows, n_fields, n_cells = cloud_state.shape
    n_vars, lev_dev, n_nodes = host_state.shape
    n_cols = substeps.shape[0]
    elem_dev = n_nodes // 16
    cell_width = CRM_X
    lev_at = lax.axis_index("lev")
    node_ids = jnp.arange(n_nodes)
    column_of_node = node_ids // 16 * 4 + node_ids // 4 % 4 // 2 * 2 + node_ids % 4 // 2
    member = (column_of_node[:, None] == jnp.arange(n_cols)[None, :]).astype(jnp.float32)
    pooling = 0.25 * member
    host_flat = host_state.reshape(n_vars * lev_dev, n_nodes)
    host_columns = (
        jnp.dot(host_flat, pooling, precision=highest)
        .reshape(n_vars, lev_dev, n_cols)
        .transpose(2, 0, 1)
    )
    every_host = lax.all_gather(host_columns, "lev", axis=2, tiled=True)
    whole_host = lax.dynamic_slice_in_dim(every_host, lev_at * own_rows, own_rows, 0)
    driving = jnp.einsum("fv,nvl->nfl", force_map, whole_host, precision=highest)
    own_counts = lax.dynamic_slice_in_dim(substeps, lev_at * own_rows, own_rows, 0)
    cloud_new = advance_clouds(cloud_state, driving, own_counts, field_coupling)
    n_levels = n_cells // cell_width
    change = (
        (cloud_new - cloud_state).reshape(own_rows, n_fields, n_levels, cell_width).mean(axis=3)
    )
    every_change = lax.all_gather(change, "lev", axis=0, tiled=True)
    level_change = lax.dynamic_slice_in_dim(every_change, lev_at * lev_dev, lev_dev, 2)
    column_tendency = jnp.einsum("vf,nfl->vln", feedback_map, level_change, precision=highest)
    physics = jnp.dot(
        column_tendency.reshape(n_vars * lev_dev, n_cols), member.T, precision=highest
    ).reshape(n_vars, lev_dev, n_nodes)
    derivative = gll_derivative()
    kron_x = jnp.asarray(np.kron(np.eye(elem_dev * 4), derivative).T, jnp.float32)
    kron_y = jnp.asarray(np.kron(np.eye(elem_dev), np.kron(derivative, np.eye(4))).T, jnp.float32)

    def tendency(field):
        flat = field.reshape(n_vars * lev_dev, n_nodes)
        along_x = jnp.dot(flat, kron_x, precision=highest).reshape(field.shape)
        along_y = jnp.dot(flat, kron_y, precision=highest).reshape(field.shape)
        padded = padded_2(field, (("lev", 1),), 1, False)
        return (
            -(wind_field[0] * along_x + wind_field[1] * along_y)
            + host_mix * (padded[:, 2:] + padded[:, :-2] - 2.0 * field)
            + physics
        )

    tables = edge_tables(element_links, n_nodes)
    mass_total = edge_sum(node_mass.reshape(1, 1, n_nodes), tables)

    def smooth(values):
        return edge_sum(node_mass * values, tables) / mass_total

    first_section = smooth(host_state + host_step * tendency(host_state))
    second_section = smooth(
        0.75 * host_state + 0.25 * (first_section + host_step * tendency(first_section))
    )
    host_new = smooth(
        host_state / 3.0 + 2.0 / 3.0 * (second_section + host_step * tendency(second_section))
    )
    return (cloud_new, host_new)


def solution(mesh):
    placed = (
        P(("elem", "lev"), None, None),
        P("elem"),
        P("elem", None),
        P(None, "lev", "elem"),
        P(None, "lev", "elem"),
        P("elem"),
        P(),
        P(),
        P(),
    )
    return jax.shard_map(
        shards,
        mesh=mesh,
        in_specs=placed,
        out_specs=(P(("elem", "lev"), None, None), P(None, "lev", "elem")),
        check_vma=False,
    )
```

profile of v0, /device:TPU:230, one launch (start us, length us, event | category | flops | bytes accessed | tf_op | source)
XLA Modules:
  0.0 390.2 jit_solution(18212692638045972472)
XLA Ops:
  1.7 5.4 %collective-permute-start.4 = (f32[1,1,256]{2,1,0:T(1,128)S(1)}, f32[1,1,256]{2,1,0:T(1,128)S(1)}, u32[]{:S(2)}, u32[]{:S(2)}) collective-permute-start(f32[1,1,256]{2,1,0:T(1,128)S(1)} %convolution_bitcast_fusion.4), channel_id=1, source_target_pairs={{0,16},{16,32},{32,48},{48,64},{64,80},{80,96},{96,112},{112,128},... | collective-permute-start | bytes 3080 | tf_op jit(solution)/shard_map/ppermute | solution.py:24
  30.8 15.3 %all_gather.6 = f32[128,4,64]{0,1,2:T(4,128)S(1)} all-gather(f32[128,4,4]{0,1,2:T(4,128)S(1)} %bitcast.238), channel_id=1, replica_groups=mesh['elem'=32,'lev'=16] {'lev'}, dimensions={2}, use_global_device_ids=true | all-gather | bytes 139264 | tf_op jit(solution)/shard_map/all_gather | solution.py:150
  48.0 68.8 %while.13 = (s32[]{:T(128)}, f32[8,8,4096]{2,1,0:T(8,128)S(1)}, s32[]{:T(128)}, s32[8]{0:T(128)S(1)}, f32[8,8]{1,0:T(8,128)S(1)}, /*index=5*/f32[8,8,64]{2,1,0:T(8,128)S(1)}, s32[]{:T(128)}) while((s32[]{:T(128)}, f32[8,8,4096]{2,1,0:T(8,128)S(1)}, s32[]{:T(128)}, s32[8]{0:T(128)S(1)}, f32[8,8]{1,0:T(8,128)S(1)}, ...), condition=%wide.region_2.3_spmd.clone, body=%wide.region_1.2_spmd.clone.sunk | while | flops 28835848 | bytes 22041208 | solution.py:76
  56.1 3.2 fusion.176
  67.5 3.2 fusion.176
  78.8 3.2 fusion.176
  90.2 3.2 fusion.176
  101.5 3.2 fusion.176
  112.9 3.2 fusion.176
  123.1 17.1 %all_gather.7 = f32[128,8,64]{2,1,0:T(8,128)S(1)} all-gather(f32[8,8,64]{2,1,0:T(8,128)S(1)} %broadcast_multiply_fusion), channel_id=1, replica_groups=mesh['elem'=32,'lev'=16] {'lev'}, dimensions={0}, use_global_device_ids=true | all-gather | bytes 278528 | tf_op jit(solution)/shard_map/all_gather | solution.py:159
  141.9 4.2 %select_select_fusion.3 = s32[512,1]{0,1:T(1,128)S(1)} fusion(s32[]{:T(128)} %bitcast.40, s32[]{:T(128)} %bitcast.41, s32[]{:T(128)} %bitcast.42, s32[]{:T(128)} %bitcast.43, s32[]{:T(128)} %bitcast.44, s32[]{:T(128)} %bitcast.46, s32[]{:T(128)} %bitcast.45), kind=kLoop, calls=%fused_computation.216 | loop fusion | flops 11776 | bytes 2076 | tf_op jit(solution)/shard_map/gather | solution.py:91
  146.1 4.4 %select_select_fusion.2 = s32[512,1]{0,1:T(1,128)S(1)} fusion(s32[]{:T(128)} %bitcast.73, s32[]{:T(128)} %bitcast.74, s32[]{:T(128)} %bitcast.75, s32[]{:T(128)} %bitcast.76, s32[]{:T(128)} %bitcast.77, s32[]{:T(128)} %bitcast.79, s32[]{:T(128)} %bitcast.78), kind=kLoop, calls=%fused_computation.215 | loop fusion | flops 11776 | bytes 2076 | tf_op jit(solution)/shard_map/gather | solution.py:92
  150.4 4.4 %select_select_fusion.1 = s32[512,1]{0,1:T(1,128)S(1)} fusion(s32[]{:T(128)} %bitcast.106, s32[]{:T(128)} %bitcast.107, s32[]{:T(128)} %bitcast.108, s32[]{:T(128)} %bitcast.109, s32[]{:T(128)} %bitcast.110, s32[]{:T(128)} %bitcast.112, s32[]{:T(128)} %bitcast.111), kind=kLoop, calls=%fused_computation.214 | loop fusion | flops 11776 | bytes 2076 | tf_op jit(solution)/shard_map/gather | solution.py:101
  154.9 4.5 %select_select_fusion = s32[512,1]{0,1:T(1,128)S(1)} fusion(s32[]{:T(128)} %bitcast.139, s32[]{:T(128)} %bitcast.140, s32[]{:T(128)} %bitcast.141, s32[]{:T(128)} %bitcast.142, s32[]{:T(128)} %bitcast.143, s32[]{:T(128)} %bitcast.145, s32[]{:T(128)} %bitcast.144), kind=kLoop, calls=%fused_computation.213 | loop fusion | flops 11776 | bytes 2076 | tf_op jit(solution)/shard_map/gather | solution.py:102
  159.3 30.8 %fusion.104 = s32[512]{0:T(512)S(1)} fusion(pred[512]{0:T(512)(128)(4,1)S(1)} %compare_reduce_fusion, pred[512]{0:T(512)(128)(4,1)S(1)} %compare_reduce_fusion.1, pred[512]{0:T(512)(128)(4,1)S(1)} %compare_reduce_fusion.2, pred[512]{0:T(512)(128)(4,1)S(1)} %compare_reduce_fusion.3, pred[512]{0:T(512)(128)(4,1)S(1)} %compare_reduce_fusion.4, ...), kind=kLoop, calls=%fused_computation.204 | loop fusion | flops 53248 | bytes 19144 | tf_op jit(solution)/shard_map/jit(_where)/select_n | solution.py:105
  190.2 31.2 %fusion.94 = s32[512]{0:T(512)S(1)} fusion(pred[512]{0:T(512)(128)(4,1)S(1)} %compare_reduce_fusion, pred[512]{0:T(512)(128)(4,1)S(1)} %compare_reduce_fusion.1, pred[512]{0:T(512)(128)(4,1)S(1)} %compare_reduce_fusion.2, pred[512]{0:T(512)(128)(4,1)S(1)} %compare_reduce_fusion.3, pred[512]{0:T(512)(128)(4,1)S(1)} %compare_reduce_fusion.4, ...), kind=kLoop, calls=%fused_computation.194 | loop fusion | flops 64512 | bytes 19148 | tf_op jit(solution)/shard_map/jit(_where)/select_n | solution.py:97
  223.1 7.2 %collective-permute-start.2 = (f32[4,4,256]{2,1,0:T(4,128)S(1)}, f32[4,4,256]{2,1,0:T(4,128)S(1)}, u32[]{:S(2)}, u32[]{:S(2)}) collective-permute-start(f32[4,4,256]{2,1,0:T(4,128)S(1)} %fusion.37), channel_id=1, source_target_pairs={{0,16},{16,32},{32,48},{48,64},{64,80},{80,96},{96,112},{112,128},... | collective-permute-start | bytes 49160 | tf_op jit(solution)/shard_map/ppermute | solution.py:24
  232.7 6.6 %collective-permute-done.3 = f32[4,4,256]{2,1,0:T(4,128)S(1)} collective-permute-done((f32[4,4,256]{2,1,0:T(4,128)S(1)}, f32[4,4,256]{2,1,0:T(4,128)S(1)}, u32[]{:S(2)}, u32[]{:S(2)}) %collective-permute-start.3) | collective-permute-done | bytes 16416 | tf_op jit(solution)/shard_map/ppermute | solution.py:26
  242.3 2.4 collective-permute-start.7
  245.4 3.1 collective-permute-done.7
  251.4 104.3 %collective-permute-start.9 = (f32[4,4,256]{2,1,0:T(4,128)S(1)}, f32[4,4,256]{2,1,0:T(4,128)S(1)}, u32[]{:S(2)}, u32[]{:S(2)}) collective-permute-start(f32[4,4,256]{2,1,0:T(4,128)S(1)} %fusion.35), channel_id=1, source_target_pairs={{16,0},{32,16},{48,32},{64,48},{80,64},{96,80},{112,96},{128,112},... | collective-permute-start | bytes 49160 | tf_op jit(solution)/shard_map/ppermute | solution.py:26
  363.2 3.1 collective-permute-done.11
  367.3 12.3 %collective-permute-start.12 = (f32[4,4,256]{2,1,0:T(4,128)S(1)}, f32[4,4,256]{2,1,0:T(4,128)S(1)}, u32[]{:S(2)}, u32[]{:S(2)}) collective-permute-start(f32[4,4,256]{2,1,0:T(4,128)S(1)} %fusion.33), channel_id=1, source_target_pairs={{0,16},{16,32},{32,48},{48,64},{64,80},{80,96},{96,112},{112,128},... | collective-permute-start | bytes 49160 | tf_op jit(solution)/shard_map/ppermute | solution.py:24
  381.5 7.0 %collective-permute-done.13 = f32[4,4,256]{2,1,0:T(4,128)S(1)} collective-permute-done((f32[4,4,256]{2,1,0:T(4,128)S(1)}, f32[4,4,256]{2,1,0:T(4,128)S(1)}, u32[]{:S(2)}, u32[]{:S(2)}) %collective-permute-start.13) | collective-permute-done | bytes 16416 | tf_op jit(solution)/shard_map/ppermute | solution.py:26
  (183 shorter events, 101.5 us)
Async XLA Ops:
  0.6 47.1 %copy-start = (f32[8,4]{0,1:T(4,128)S(1)}, f32[8,4]{0,1:T(4,128)}, u32[]{:S(2)}) copy-start(f32[8,4]{0,1:T(4,128)} %param.20) | copy-start | bytes 388
  0.6 47.3 %copy-start.2 = (f32[8,8,4096]{2,1,0:T(8,128)S(1)}, f32[8,8,4096]{2,1,0:T(8,128)}, u32[]{:S(2)}) copy-start(f32[8,8,4096]{2,1,0:T(8,128)} %param.13) | copy-start | bytes 3145732
  0.7 47.3 %copy-start.6 = (f32[8,8]{1,0:T(8,128)S(1)}, f32[8,8]{1,0:T(8,128)}, u32[]{:S(2)}) copy-start(f32[8,8]{1,0:T(8,128)} %param.19) | copy-start | bytes 772
  1.7 219.8 %collective-permute-start.4 = (f32[1,1,256]{2,1,0:T(1,128)S(1)}, f32[1,1,256]{2,1,0:T(1,128)S(1)}, u32[]{:S(2)}, u32[]{:S(2)}) collective-permute-start(f32[1,1,256]{2,1,0:T(1,128)S(1)} %convolution_bitcast_fusion.4), channel_id=1, source_target_pairs={{0,16},{16,32},{32,48},{48,64},{64,80},{80,96},{96,112},{112,128},... | collective-permute-start | bytes 3080 | tf_op jit(solution)/shard_map/ppermute | solution.py:24
  7.1 214.3 %collective-permute-start.5 = (f32[1,1,256]{2,1,0:T(1,128)S(1)}, f32[1,1,256]{2,1,0:T(1,128)S(1)}, u32[]{:S(2)}, u32[]{:S(2)}) collective-permute-start(f32[1,1,256]{2,1,0:T(1,128)S(1)} %convolution_bitcast_fusion.4), channel_id=1, source_target_pairs={{16,0},{32,16},{48,32},{64,48},{80,64},{96,80},{112,96},{128,112},... | collective-permute-start | bytes 3080 | tf_op jit(solution)/shard_map/ppermute | solution.py:26
  9.9 212.1 %collective-permute-start = (f32[4,1,512]{2,1,0:T(1,128)S(1)}, f32[4,1,512]{2,1,0:T(1,128)S(1)}, u32[]{:S(2)}, u32[]{:S(2)}) collective-permute-start(f32[4,1,512]{2,1,0:T(1,128)S(1)} %get-tuple-element.121), channel_id=1, source_target_pairs={{1,0},{2,1},{3,2},{4,3},{5,4},{6,5},{7,6},{8,7},{9,8},{10,9},{11,1... | collective-permute-start | bytes 24584 | tf_op jit(solution)/shard_map/ppermute | solution.py:26
  11.8 210.2 %collective-permute-start.1 = (f32[4,1,512]{2,1,0:T(1,128)S(1)}, f32[4,1,512]{2,1,0:T(1,128)S(1)}, u32[]{:S(2)}, u32[]{:S(2)}) collective-permute-start(f32[4,1,512]{2,1,0:T(1,128)S(1)} %get-tuple-element.122), channel_id=1, source_target_pairs={{0,1},{1,2},{2,3},{3,4},{4,5},{5,6},{6,7},{7,8},{8,9},{9,10},{10,1... | collective-permute-start | bytes 24584 | tf_op jit(solution)/shard_map/ppermute | solution.py:24
  116.7 4.0 %copy-start.1 = (f32[8,8,4096]{2,1,0:T(8,128)}, f32[8,8,4096]{2,1,0:T(8,128)S(1)}, u32[]{:S(2)}) copy-start(f32[8,8,4096]{2,1,0:T(8,128)S(1)} %get-tuple-element.80) | copy-start | bytes 3145732
  120.7 19.9 %copy-start.9 = (f32[4,8]{1,0:T(4,128)S(1)}, f32[4,8]{1,0:T(4,128)}, u32[]{:S(2)}) copy-start(f32[4,8]{1,0:T(4,128)} %param.21) | copy-start | bytes 388
  120.7 20.4 %copy-start.8 = (f32[2,4,512]{2,1,0:T(4,128)S(1)}, f32[2,4,512]{2,1,0:T(4,128)}, u32[]{:S(2)}) copy-start(f32[2,4,512]{2,1,0:T(4,128)} %param.17) | copy-start | bytes 49156
  120.7 20.4 %copy-start.4 = (f32[512,512,1]{1,0,2:T(8,128)S(1)}, f32[512,512,1]{1,0,2:T(8,128)}, u32[]{:S(2)}) copy-start(f32[512,512,1]{1,0,2:T(8,128)} %constant.378) | copy-start | bytes 3145732
  120.8 20.4 %copy-start.5 = (f32[4,4,512]{2,1,0:T(4,128)S(1)}, f32[4,4,512]{2,1,0:T(4,128)}, u32[]{:S(2)}) copy-start(f32[4,4,512]{2,1,0:T(4,128)} %param.16) | copy-start | bytes 98308
  123.1 98.9 %copy-start.7 = (f32[512]{0:T(512)S(1)}, f32[512]{0:T(512)}, u32[]{:S(2)}) copy-start(f32[512]{0:T(512)} %param.18) | copy-start | bytes 6148
  123.1 99.0 %copy-start.3 = (f32[512,512,1]{1,0,2:T(8,128)S(1)}, f32[512,512,1]{1,0,2:T(8,128)}, u32[]{:S(2)}) copy-start(f32[512,512,1]{1,0,2:T(8,128)} %constant.379) | copy-start | bytes 3145732
  223.1 9.6 %collective-permute-start.2 = (f32[4,4,256]{2,1,0:T(4,128)S(1)}, f32[4,4,256]{2,1,0:T(4,128)S(1)}, u32[]{:S(2)}, u32[]{:S(2)}) collective-permute-start(f32[4,4,256]{2,1,0:T(4,128)S(1)} %fusion.37), channel_id=1, source_target_pairs={{0,16},{16,32},{32,48},{48,64},{64,80},{80,96},{96,112},{112,128},... | collective-permute-start | bytes 49160 | tf_op jit(solution)/shard_map/ppermute | solution.py:24
  230.3 9.0 %collective-permute-start.3 = (f32[4,4,256]{2,1,0:T(4,128)S(1)}, f32[4,4,256]{2,1,0:T(4,128)S(1)}, u32[]{:S(2)}, u32[]{:S(2)}) collective-permute-start(f32[4,4,256]{2,1,0:T(4,128)S(1)} %fusion.37), channel_id=1, source_target_pairs={{16,0},{32,16},{48,32},{64,48},{80,64},{96,80},{112,96},{128,112},... | collective-permute-start | bytes 49160 | tf_op jit(solution)/shard_map/ppermute | solution.py:26
  240.4 5.0 %collective-permute-start.6 = (f32[4,1,512]{2,1,0:T(1,128)S(1)}, f32[4,1,512]{2,1,0:T(1,128)S(1)}, u32[]{:S(2)}, u32[]{:S(2)}) collective-permute-start(f32[4,1,512]{2,1,0:T(1,128)S(1)} %get-tuple-element.119), channel_id=1, source_target_pairs={{1,0},{2,1},{3,2},{4,3},{5,4},{6,5},{7,6},{8,7},{9,8},{10,9},{11,1... | collective-permute-start | bytes 24584 | tf_op jit(solution)/shard_map/ppermute | solution.py:26
  242.3 6.2 %collective-permute-start.7 = (f32[4,1,512]{2,1,0:T(1,128)S(1)}, f32[4,1,512]{2,1,0:T(1,128)S(1)}, u32[]{:S(2)}, u32[]{:S(2)}) collective-permute-start(f32[4,1,512]{2,1,0:T(1,128)S(1)} %get-tuple-element.120), channel_id=1, source_target_pairs={{0,1},{1,2},{2,3},{3,4},{4,5},{5,6},{6,7},{7,8},{8,9},{9,10},{10,1... | collective-permute-start | bytes 24584 | tf_op jit(solution)/shard_map/ppermute | solution.py:24
  249.5 106.2 %collective-permute-start.8 = (f32[4,4,256]{2,1,0:T(4,128)S(1)}, f32[4,4,256]{2,1,0:T(4,128)S(1)}, u32[]{:S(2)}, u32[]{:S(2)}) collective-permute-start(f32[4,4,256]{2,1,0:T(4,128)S(1)} %fusion.35), channel_id=1, source_target_pairs={{0,16},{16,32},{32,48},{48,64},{64,80},{80,96},{96,112},{112,128},... | collective-permute-start | bytes 49160 | tf_op jit(solution)/shard_map/ppermute | solution.py:24
  251.4 105.7 %collective-permute-start.9 = (f32[4,4,256]{2,1,0:T(4,128)S(1)}, f32[4,4,256]{2,1,0:T(4,128)S(1)}, u32[]{:S(2)}, u32[]{:S(2)}) collective-permute-start(f32[4,4,256]{2,1,0:T(4,128)S(1)} %fusion.35), channel_id=1, source_target_pairs={{16,0},{32,16},{48,32},{64,48},{80,64},{96,80},{112,96},{128,112},... | collective-permute-start | bytes 49160 | tf_op jit(solution)/shard_map/ppermute | solution.py:26
  358.2 5.0 %collective-permute-start.10 = (f32[4,1,512]{2,1,0:T(1,128)S(1)}, f32[4,1,512]{2,1,0:T(1,128)S(1)}, u32[]{:S(2)}, u32[]{:S(2)}) collective-permute-start(f32[4,1,512]{2,1,0:T(1,128)S(1)} %get-tuple-element.117), channel_id=1, source_target_pairs={{1,0},{2,1},{3,2},{4,3},{5,4},{6,5},{7,6},{8,7},{9,8},{10,9},{11,1... | collective-permute-start | bytes 24584 | tf_op jit(solution)/shard_map/ppermute | solution.py:26
  360.1 6.2 %collective-permute-start.11 = (f32[4,1,512]{2,1,0:T(1,128)S(1)}, f32[4,1,512]{2,1,0:T(1,128)S(1)}, u32[]{:S(2)}, u32[]{:S(2)}) collective-permute-start(f32[4,1,512]{2,1,0:T(1,128)S(1)} %get-tuple-element.118), channel_id=1, source_target_pairs={{0,1},{1,2},{2,3},{3,4},{4,5},{5,6},{6,7},{7,8},{8,9},{9,10},{10,1... | collective-permute-start | bytes 24584 | tf_op jit(solution)/shard_map/ppermute | solution.py:24
  367.3 14.2 %collective-permute-start.12 = (f32[4,4,256]{2,1,0:T(4,128)S(1)}, f32[4,4,256]{2,1,0:T(4,128)S(1)}, u32[]{:S(2)}, u32[]{:S(2)}) collective-permute-start(f32[4,4,256]{2,1,0:T(4,128)S(1)} %fusion.33), channel_id=1, source_target_pairs={{0,16},{16,32},{32,48},{48,64},{64,80},{80,96},{96,112},{112,128},... | collective-permute-start | bytes 49160 | tf_op jit(solution)/shard_map/ppermute | solution.py:24
  379.5 9.0 %collective-permute-start.13 = (f32[4,4,256]{2,1,0:T(4,128)S(1)}, f32[4,4,256]{2,1,0:T(4,128)S(1)}, u32[]{:S(2)}, u32[]{:S(2)}) collective-permute-start(f32[4,4,256]{2,1,0:T(4,128)S(1)} %fusion.33), channel_id=1, source_target_pairs={{16,0},{32,16},{48,32},{64,48},{80,64},{96,80},{112,96},{128,112},... | collective-permute-start | bytes 49160 | tf_op jit(solution)/shard_map/ppermute | solution.py:26
where the time goes:
time: 393 us; the launch traced here: 390 us
  starting transfers between devices  150 us (38%)
  other arithmetic  93.6 us (24%)
  local copies, waits for them, and re-layouts  56.8 us (14%)
  blocking collectives  32.4 us (8%)
  matrix products  29.9 us (8%)
  waiting for transfers between devices  21.2 us (5%)
  loops' own time  5.2 us (1%)
    ppermute x7, starting transfers between devices, padded_2(): lax.ppermute(head, axis, [((i + 1) % count, i) for i in range(ends)])  116 us
    ppermute x7, starting transfers between devices, padded_2(): lax.ppermute(tail, axis, [(i, (i + 1) % count) for i in range(ends)])  34.1 us
    select_n x1, other arithmetic, edge_tables(): jnp.where(col_of == 0, left_source, jnp.where(col_of == 3, right_source,...  31.2 us
    select_n x1, other arithmetic, edge_tables(): jnp.where(row_of == 0, lower_source, jnp.where(row_of == 3, upper_source,...  30.8 us
    dot_general x6, matrix products, one_step(): jnp.einsum('gf,nfc->ngc', coupling, current, precision=highest)  19 us
    all_gather x1, blocking collectives, shards(): every_change = lax.all_gather(change, 'lev', axis=0, tiled=True)  17.1 us
    all_gather x1, blocking collectives, shards(): every_host = lax.all_gather(host_columns, 'lev', axis=2, tiled=True)  15.3 us
    ppermute x7, waiting for transfers between devices, padded_2(): lax.ppermute(head, axis, [((i + 1) % count, i) for i in range(ends)])  15 us
  transfers between devices with their start and end apart: 14, of which 5 were waited for; matrix products, arithmetic and copies ran while one was open for 44% of the time, Pallas kernels for 0%

commit v1 on v0

--- a/solution.py
+++ b/solution.py
@@ -11,6 +11,14 @@
 host_step = 0.1
 host_mix = 0.2
 highest = lax.Precision.HIGHEST
+
+
+def gather_by_exchange(value, axis, dim):
+    size = lax.axis_size(axis)
+    repeats = [size if d == dim else 1 for d in range(value.ndim)]
+    return lax.all_to_all(
+        jnp.tile(value, repeats), axis, split_axis=dim, concat_axis=dim, tiled=True
+    )
 
 
 def padded_2(cells, sides, width, closed):
@@ -156,7 +164,7 @@
     change = (
         (cloud_new - cloud_state).reshape(own_rows, n_fields, n_levels, cell_width).mean(axis=3)
     )
-    every_change = lax.all_gather(change, "lev", axis=0, tiled=True)
+    every_change = gather_by_exchange(change, "lev", 0)
     level_change = lax.dynamic_slice_in_dim(every_change, lev_at * lev_dev, lev_dev, 2)
     column_tendency = jnp.einsum("vf,nfl->vln", feedback_map, level_change, precision=highest)
     physics = jnp.dot(

time: 393 us -> 378 us (0.962)
  blocking collectives: 32.4 us -> 15.1 us
  local copies, waits for them, and re-layouts: 56.8 us -> 48.4 us
  starting transfers between devices: 150 us -> 158 us
    all_gather x1 -> x0, blocking collectives: 17.1 us -> none  [shards(): every_change = lax.all_gather(change, 'lev', axis=0, tiled=True)]
    all_to_all x0 -> x1, starting transfers between devices: none -> 7.22 us  [gather_by_exchange(): lax.all_to_all(jnp.tile(value, repeats), axis, split_axis=dim, concat_axi...]
    gather x4, local copies, waits for them, and re-layouts: 8.41 us -> 2.9 us  [edge_tables(): lower_ids = element_links[:, 2][elem_of] % elem_dev]
  transfers between devices with their start and end apart: 14 -> 15, of which waited for: 5 -> 5; matrix products, arithmetic and copies ran while one was open for 44% -> 44% of each run, Pallas kernels for 0% -> 0%
where the time goes in v1:
time: 378 us; the launch traced here: 375 us
  starting transfers between devices  158 us (42%)
  other arithmetic  95.3 us (25%)
  local copies, waits for them, and re-layouts  48.4 us (13%)
  matrix products  29.9 us (8%)
  waiting for transfers between devices  21.7 us (6%)
  blocking collectives  15.1 us (4%)
  loops' own time  5.2 us (1%)
    ppermute x7, starting transfers between devices, padded_2(): lax.ppermute(head, axis, [((i + 1) % count, i) for i in range(ends)])  118 us
    ppermute x7, starting transfers between devices, padded_2(): lax.ppermute(tail, axis, [(i, (i + 1) % count) for i in range(ends)])  33.2 us
    select_n x1, other arithmetic, edge_tables(): jnp.where(col_of == 0, left_source, jnp.where(col_of == 3, right_source,...  31.2 us
    select_n x1, other arithmetic, edge_tables(): jnp.where(row_of == 0, lower_source, jnp.where(row_of == 3, upper_source,...  31.1 us
    dot_general x6, matrix products, one_step(): jnp.einsum('gf,nfc->ngc', coupling, current, precision=highest)  19 us
    all_gather x1, blocking collectives, shards(): every_host = lax.all_gather(host_columns, 'lev', axis=2, tiled=True)  15.1 us
    ppermute x7, waiting for transfers between devices, padded_2(): lax.ppermute(head, axis, [((i + 1) % count, i) for i in range(ends)])  15 us
    add x6, local copies, waits for them, and re-layouts, one_step(): eastward + westward - 2.0 * current  9.86 us
  transfers between devices with their start and end apart: 15, of which 5 were waited for; matrix products, arithmetic and copies ran while one was open for 44% of the time, Pallas kernels for 0%

profile of v1, /device:TPU:230, one launch (start us, length us, event | category | flops | bytes accessed | tf_op | source)
XLA Modules:
  0.0 375.3 jit_solution(10210923903399305241)
XLA Ops:
  1.7 5.4 %collective-permute-start.4 = (f32[1,1,256]{2,1,0:T(1,128)S(1)}, f32[1,1,256]{2,1,0:T(1,128)S(1)}, u32[]{:S(2)}, u32[]{:S(2)}) collective-permute-start(f32[1,1,256]{2,1,0:T(1,128)S(1)} %convolution_bitcast_fusion.4), channel_id=1, source_target_pairs={{0,16},{16,32},{32,48},{48,64},{64,80},{80,96},{96,112},{112,128},... | collective-permute-start | bytes 3080 | tf_op jit(solution)/shard_map/ppermute | solution.py:32
  10.2 15.1 %all_gather.3 = f32[128,4,64]{0,1,2:T(4,128)S(1)} all-gather(f32[128,4,4]{0,1,2:T(4,128)S(1)} %bitcast.240), channel_id=1, replica_groups=mesh['elem'=32,'lev'=16] {'lev'}, dimensions={2}, use_global_device_ids=true | all-gather | bytes 139264 | tf_op jit(solution)/shard_map/all_gather | solution.py:158
  27.3 68.8 %while.13 = (s32[]{:T(128)}, f32[8,8,4096]{2,1,0:T(8,128)S(1)}, s32[]{:T(128)}, s32[8]{0:T(128)S(1)}, f32[8,8]{1,0:T(8,128)S(1)}, /*index=5*/f32[8,8,64]{2,1,0:T(8,128)S(1)}, s32[]{:T(128)}) while((s32[]{:T(128)}, f32[8,8,4096]{2,1,0:T(8,128)S(1)}, s32[]{:T(128)}, s32[8]{0:T(128)S(1)}, f32[8,8]{1,0:T(8,128)S(1)}, ...), condition=%wide.region_2.3_spmd.clone, body=%wide.region_1.2_spmd.clone.sunk | while | flops 28835848 | bytes 22041208 | solution.py:84
  35.5 3.2 fusion.176
  46.8 3.2 fusion.176
  58.1 3.2 fusion.176
  69.5 3.2 fusion.176
  80.8 3.2 fusion.176
  92.2 3.2 fusion.176
  103.5 7.2 %all-to-all-start = ((f32[16,1,4096]{2,1,0:T(1,128)}), f32[16,1,4096]{2,1,0:T(1,128)S(1)}, u32[]{:S(2)}, u32[]{:S(2)}) async-start(f32[16,1,4096]{2,1,0:T(1,128)} %reshape.1001), calls=%async_computation | async-start | bytes 524288 | tf_op jit(solution)/shard_map/all_to_all | solution.py:19
  122.0 4.4 %select_select_fusion.3 = s32[512,1]{0,1:T(1,128)S(1)} fusion(s32[]{:T(128)} %bitcast.41, s32[]{:T(128)} %bitcast.42, s32[]{:T(128)} %bitcast.43, s32[]{:T(128)} %bitcast.44, s32[]{:T(128)} %bitcast.45, s32[]{:T(128)} %bitcast.47, s32[]{:T(128)} %bitcast.46), kind=kLoop, calls=%fused_computation.216 | loop fusion | flops 11776 | bytes 2076 | tf_op jit(solution)/shard_map/gather | solution.py:99
  126.4 4.5 %select_select_fusion.1 = s32[512,1]{0,1:T(1,128)S(1)} fusion(s32[]{:T(128)} %bitcast.107, s32[]{:T(128)} %bitcast.108, s32[]{:T(128)} %bitcast.109, s32[]{:T(128)} %bitcast.110, s32[]{:T(128)} %bitcast.111, s32[]{:T(128)} %bitcast.113, s32[]{:T(128)} %bitcast.112), kind=kLoop, calls=%fused_computation.214 | loop fusion | flops 11776 | bytes 2076 | tf_op jit(solution)/shard_map/gather | solution.py:109
  130.9 4.4 %select_select_fusion = s32[512,1]{0,1:T(1,128)S(1)} fusion(s32[]{:T(128)} %bitcast.140, s32[]{:T(128)} %bitcast.141, s32[]{:T(128)} %bitcast.142, s32[]{:T(128)} %bitcast.143, s32[]{:T(128)} %bitcast.144, s32[]{:T(128)} %bitcast.146, s32[]{:T(128)} %bitcast.145), kind=kLoop, calls=%fused_computation.213 | loop fusion | flops 11776 | bytes 2076 | tf_op jit(solution)/shard_map/gather | solution.py:110
  135.3 31.1 %fusion.104 = s32[512]{0:T(512)S(1)} fusion(pred[512]{0:T(512)(128)(4,1)S(1)} %compare_reduce_fusion, pred[512]{0:T(512)(128)(4,1)S(1)} %compare_reduce_fusion.1, pred[512]{0:T(512)(128)(4,1)S(1)} %compare_reduce_fusion.2, pred[512]{0:T(512)(128)(4,1)S(1)} %compare_reduce_fusion.3, pred[512]{0:T(512)(128)(4,1)S(1)} %compare_reduce_fusion.4, ...), kind=kLoop, calls=%fused_computation.204 | loop fusion | flops 53248 | bytes 19144 | tf_op jit(solution)/shard_map/jit(_where)/select_n | solution.py:113
  166.4 4.4 %select_select_fusion.2 = s32[512,1]{0,1:T(1,128)S(1)} fusion(s32[]{:T(128)} %bitcast.74, s32[]{:T(128)} %bitcast.75, s32[]{:T(128)} %bitcast.76, s32[]{:T(128)} %bitcast.77, s32[]{:T(128)} %bitcast.78, s32[]{:T(128)} %bitcast.80, s32[]{:T(128)} %bitcast.79), kind=kLoop, calls=%fused_computation.215 | loop fusion | flops 11776 | bytes 2076 | tf_op jit(solution)/shard_map/gather | solution.py:100
  170.8 31.2 %fusion.94 = s32[512]{0:T(512)S(1)} fusion(pred[512]{0:T(512)(128)(4,1)S(1)} %compare_reduce_fusion, pred[512]{0:T(512)(128)(4,1)S(1)} %compare_reduce_fusion.1, pred[512]{0:T(512)(128)(4,1)S(1)} %compare_reduce_fusion.2, pred[512]{0:T(512)(128)(4,1)S(1)} %compare_reduce_fusion.3, pred[512]{0:T(512)(128)(4,1)S(1)} %compare_reduce_fusion.4, ...), kind=kLoop, calls=%fused_computation.194 | loop fusion | flops 64512 | bytes 19148 | tf_op jit(solution)/shard_map/jit(_where)/select_n | solution.py:105
  206.6 7.2 %collective-permute-start.2 = (f32[4,4,256]{2,1,0:T(4,128)S(1)}, f32[4,4,256]{2,1,0:T(4,128)S(1)}, u32[]{:S(2)}, u32[]{:S(2)}) collective-permute-start(f32[4,4,256]{2,1,0:T(4,128)S(1)} %fusion.37), channel_id=1, source_target_pairs={{0,16},{16,32},{32,48},{48,64},{64,80},{80,96},{96,112},{112,128},... | collective-permute-start | bytes 49160 | tf_op jit(solution)/shard_map/ppermute | solution.py:32
  216.2 6.6 %collective-permute-done.3 = f32[4,4,256]{2,1,0:T(4,128)S(1)} collective-permute-done((f32[4,4,256]{2,1,0:T(4,128)S(1)}, f32[4,4,256]{2,1,0:T(4,128)S(1)}, u32[]{:S(2)}, u32[]{:S(2)}) %collective-permute-start.3) | collective-permute-done | bytes 16416 | tf_op jit(solution)/shard_map/ppermute | solution.py:34
  224.0 3.1 collective-permute-start.6
  229.7 3.6 collective-permute-done.7
  236.2 104.8 %collective-permute-start.9 = (f32[4,4,256]{2,1,0:T(4,128)S(1)}, f32[4,4,256]{2,1,0:T(4,128)S(1)}, u32[]{:S(2)}, u32[]{:S(2)}) collective-permute-start(f32[4,4,256]{2,1,0:T(4,128)S(1)} %fusion.35), channel_id=1, source_target_pairs={{16,0},{32,16},{48,32},{64,48},{80,64},{96,80},{112,96},{128,112},... | collective-permute-start | bytes 49160 | tf_op jit(solution)/shard_map/ppermute | solution.py:34
  348.6 3.1 collective-permute-done.11
  352.6 12.0 %collective-permute-start.12 = (f32[4,4,256]{2,1,0:T(4,128)S(1)}, f32[4,4,256]{2,1,0:T(4,128)S(1)}, u32[]{:S(2)}, u32[]{:S(2)}) collective-permute-start(f32[4,4,256]{2,1,0:T(4,128)S(1)} %fusion.33), channel_id=1, source_target_pairs={{0,16},{16,32},{32,48},{48,64},{64,80},{80,96},{96,112},{112,128},... | collective-permute-start | bytes 49160 | tf_op jit(solution)/shard_map/ppermute | solution.py:32
  366.6 7.0 %collective-permute-done.13 = f32[4,4,256]{2,1,0:T(4,128)S(1)} collective-permute-done((f32[4,4,256]{2,1,0:T(4,128)S(1)}, f32[4,4,256]{2,1,0:T(4,128)S(1)}, u32[]{:S(2)}, u32[]{:S(2)}) %collective-permute-start.13) | collective-permute-done | bytes 16416 | tf_op jit(solution)/shard_map/ppermute | solution.py:34
  (191 shorter events, 94.5 us)
Async XLA Ops:
  0.6 26.4 %copy-start = (f32[8,4]{0,1:T(4,128)S(1)}, f32[8,4]{0,1:T(4,128)}, u32[]{:S(2)}) copy-start(f32[8,4]{0,1:T(4,128)} %param.20) | copy-start | bytes 388
  0.6 26.6 %copy-start.2 = (f32[8,8,4096]{2,1,0:T(8,128)S(1)}, f32[8,8,4096]{2,1,0:T(8,128)}, u32[]{:S(2)}) copy-start(f32[8,8,4096]{2,1,0:T(8,128)} %param.13) | copy-start | bytes 3145732
  0.7 26.6 %copy-start.7 = (f32[8,8]{1,0:T(8,128)S(1)}, f32[8,8]{1,0:T(8,128)}, u32[]{:S(2)}) copy-start(f32[8,8]{1,0:T(8,128)} %param.19) | copy-start | bytes 772
  1.7 200.3 %collective-permute-start.4 = (f32[1,1,256]{2,1,0:T(1,128)S(1)}, f32[1,1,256]{2,1,0:T(1,128)S(1)}, u32[]{:S(2)}, u32[]{:S(2)}) collective-permute-start(f32[1,1,256]{2,1,0:T(1,128)S(1)} %convolution_bitcast_fusion.4), channel_id=1, source_target_pairs={{0,16},{16,32},{32,48},{48,64},{64,80},{80,96},{96,112},{112,128},... | collective-permute-start | bytes 3080 | tf_op jit(solution)/shard_map/ppermute | solution.py:32
  7.1 194.9 %collective-permute-start.5 = (f32[1,1,256]{2,1,0:T(1,128)S(1)}, f32[1,1,256]{2,1,0:T(1,128)S(1)}, u32[]{:S(2)}, u32[]{:S(2)}) collective-permute-start(f32[1,1,256]{2,1,0:T(1,128)S(1)} %convolution_bitcast_fusion.4), channel_id=1, source_target_pairs={{16,0},{32,16},{48,32},{64,48},{80,64},{96,80},{112,96},{128,112},... | collective-permute-start | bytes 3080 | tf_op jit(solution)/shard_map/ppermute | solution.py:34
  100.0 15.2 %copy-start.5 = (s32[32,4]{0,1:T(4,128)S(1)}, s32[32,4]{0,1:T(4,128)}, u32[]{:S(2)}) copy-start(s32[32,4]{0,1:T(4,128)} %param.15) | copy-start | bytes 1540
  100.0 21.1 %copy-start.9 = (f32[2,4,512]{2,1,0:T(4,128)S(1)}, f32[2,4,512]{2,1,0:T(4,128)}, u32[]{:S(2)}) copy-start(f32[2,4,512]{2,1,0:T(4,128)} %param.17) | copy-start | bytes 49156
  100.1 21.2 %copy-start.4 = (f32[512,512,1]{1,0,2:T(8,128)S(1)}, f32[512,512,1]{1,0,2:T(8,128)}, u32[]{:S(2)}) copy-start(f32[512,512,1]{1,0,2:T(8,128)} %constant.378) | copy-start | bytes 3145732
  102.4 100.2 %copy-start.8 = (f32[512]{0:T(512)S(1)}, f32[512]{0:T(512)}, u32[]{:S(2)}) copy-start(f32[512]{0:T(512)} %param.18) | copy-start | bytes 6148
  103.5 99.2 %all-to-all-start = ((f32[16,1,4096]{2,1,0:T(1,128)}), f32[16,1,4096]{2,1,0:T(1,128)S(1)}, u32[]{:S(2)}, u32[]{:S(2)}) async-start(f32[16,1,4096]{2,1,0:T(1,128)} %reshape.1001), calls=%async_computation | async-start | bytes 524288 | tf_op jit(solution)/shard_map/all_to_all | solution.py:19
  110.7 94.8 %collective-permute-start = (f32[4,1,512]{2,1,0:T(1,128)S(1)}, f32[4,1,512]{2,1,0:T(1,128)S(1)}, u32[]{:S(2)}, u32[]{:S(2)}) collective-permute-start(f32[4,1,512]{2,1,0:T(1,128)S(1)} %get-tuple-element.121), channel_id=1, source_target_pairs={{1,0},{2,1},{3,2},{4,3},{5,4},{6,5},{7,6},{8,7},{9,8},{10,9},{11,1... | collective-permute-start | bytes 24584 | tf_op jit(solution)/shard_map/ppermute | solution.py:34
  112.9 92.7 %collective-permute-start.1 = (f32[4,1,512]{2,1,0:T(1,128)S(1)}, f32[4,1,512]{2,1,0:T(1,128)S(1)}, u32[]{:S(2)}, u32[]{:S(2)}) collective-permute-start(f32[4,1,512]{2,1,0:T(1,128)S(1)} %get-tuple-element.122), channel_id=1, source_target_pairs={{0,1},{1,2},{2,3},{3,4},{4,5},{5,6},{6,7},{7,8},{8,9},{9,10},{10,1... | collective-permute-start | bytes 24584 | tf_op jit(solution)/shard_map/ppermute | solution.py:32
  122.0 83.1 %copy-start.10 = (f32[4,8]{1,0:T(4,128)S(1)}, f32[4,8]{1,0:T(4,128)}, u32[]{:S(2)}) copy-start(f32[4,8]{1,0:T(4,128)} %param.21) | copy-start | bytes 388
  122.0 83.6 %copy-start.3 = (f32[512,512,1]{1,0,2:T(8,128)S(1)}, f32[512,512,1]{1,0,2:T(8,128)}, u32[]{:S(2)}) copy-start(f32[512,512,1]{1,0,2:T(8,128)} %constant.379) | copy-start | bytes 3145732
  206.6 9.6 %collective-permute-start.2 = (f32[4,4,256]{2,1,0:T(4,128)S(1)}, f32[4,4,256]{2,1,0:T(4,128)S(1)}, u32[]{:S(2)}, u32[]{:S(2)}) collective-permute-start(f32[4,4,256]{2,1,0:T(4,128)S(1)} %fusion.37), channel_id=1, source_target_pairs={{0,16},{16,32},{32,48},{48,64},{64,80},{80,96},{96,112},{112,128},... | collective-permute-start | bytes 49160 | tf_op jit(solution)/shard_map/ppermute | solution.py:32
  213.9 9.0 %collective-permute-start.3 = (f32[4,4,256]{2,1,0:T(4,128)S(1)}, f32[4,4,256]{2,1,0:T(4,128)S(1)}, u32[]{:S(2)}, u32[]{:S(2)}) collective-permute-start(f32[4,4,256]{2,1,0:T(4,128)S(1)} %fusion.37), channel_id=1, source_target_pairs={{16,0},{32,16},{48,32},{64,48},{80,64},{96,80},{112,96},{128,112},... | collective-permute-start | bytes 49160 | tf_op jit(solution)/shard_map/ppermute | solution.py:34
  224.0 5.7 %collective-permute-start.6 = (f32[4,1,512]{2,1,0:T(1,128)S(1)}, f32[4,1,512]{2,1,0:T(1,128)S(1)}, u32[]{:S(2)}, u32[]{:S(2)}) collective-permute-start(f32[4,1,512]{2,1,0:T(1,128)S(1)} %get-tuple-element.119), channel_id=1, source_target_pairs={{1,0},{2,1},{3,2},{4,3},{5,4},{6,5},{7,6},{8,7},{9,8},{10,9},{11,1... | collective-permute-start | bytes 24584 | tf_op jit(solution)/shard_map/ppermute | solution.py:34
  227.1 6.2 %collective-permute-start.7 = (f32[4,1,512]{2,1,0:T(1,128)S(1)}, f32[4,1,512]{2,1,0:T(1,128)S(1)}, u32[]{:S(2)}, u32[]{:S(2)}) collective-permute-start(f32[4,1,512]{2,1,0:T(1,128)S(1)} %get-tuple-element.120), channel_id=1, source_target_pairs={{0,1},{1,2},{2,3},{3,4},{4,5},{5,6},{6,7},{7,8},{8,9},{9,10},{10,1... | collective-permute-start | bytes 24584 | tf_op jit(solution)/shard_map/ppermute | solution.py:32
  234.3 106.8 %collective-permute-start.8 = (f32[4,4,256]{2,1,0:T(4,128)S(1)}, f32[4,4,256]{2,1,0:T(4,128)S(1)}, u32[]{:S(2)}, u32[]{:S(2)}) collective-permute-start(f32[4,4,256]{2,1,0:T(4,128)S(1)} %fusion.35), channel_id=1, source_target_pairs={{0,16},{16,32},{32,48},{48,64},{64,80},{80,96},{96,112},{112,128},... | collective-permute-start | bytes 49160 | tf_op jit(solution)/shard_map/ppermute | solution.py:32
  236.2 106.3 %collective-permute-start.9 = (f32[4,4,256]{2,1,0:T(4,128)S(1)}, f32[4,4,256]{2,1,0:T(4,128)S(1)}, u32[]{:S(2)}, u32[]{:S(2)}) collective-permute-start(f32[4,4,256]{2,1,0:T(4,128)S(1)} %fusion.35), channel_id=1, source_target_pairs={{16,0},{32,16},{48,32},{64,48},{80,64},{96,80},{112,96},{128,112},... | collective-permute-start | bytes 49160 | tf_op jit(solution)/shard_map/ppermute | solution.py:34
  343.6 5.0 %collective-permute-start.10 = (f32[4,1,512]{2,1,0:T(1,128)S(1)}, f32[4,1,512]{2,1,0:T(1,128)S(1)}, u32[]{:S(2)}, u32[]{:S(2)}) collective-permute-start(f32[4,1,512]{2,1,0:T(1,128)S(1)} %get-tuple-element.117), channel_id=1, source_target_pairs={{1,0},{2,1},{3,2},{4,3},{5,4},{6,5},{7,6},{8,7},{9,8},{10,9},{11,1... | collective-permute-start | bytes 24584 | tf_op jit(solution)/shard_map/ppermute | solution.py:34
  345.5 6.2 %collective-permute-start.11 = (f32[4,1,512]{2,1,0:T(1,128)S(1)}, f32[4,1,512]{2,1,0:T(1,128)S(1)}, u32[]{:S(2)}, u32[]{:S(2)}) collective-permute-start(f32[4,1,512]{2,1,0:T(1,128)S(1)} %get-tuple-element.118), channel_id=1, source_target_pairs={{0,1},{1,2},{2,3},{3,4},{4,5},{5,6},{6,7},{7,8},{8,9},{9,10},{10,1... | collective-permute-start | bytes 24584 | tf_op jit(solution)/shard_map/ppermute | solution.py:32
  352.6 13.9 %collective-permute-start.12 = (f32[4,4,256]{2,1,0:T(4,128)S(1)}, f32[4,4,256]{2,1,0:T(4,128)S(1)}, u32[]{:S(2)}, u32[]{:S(2)}) collective-permute-start(f32[4,4,256]{2,1,0:T(4,128)S(1)} %fusion.33), channel_id=1, source_target_pairs={{0,16},{16,32},{32,48},{48,64},{64,80},{80,96},{96,112},{112,128},... | collective-permute-start | bytes 49160 | tf_op jit(solution)/shard_map/ppermute | solution.py:32
  364.6 9.0 %collective-permute-start.13 = (f32[4,4,256]{2,1,0:T(4,128)S(1)}, f32[4,4,256]{2,1,0:T(4,128)S(1)}, u32[]{:S(2)}, u32[]{:S(2)}) collective-permute-start(f32[4,4,256]{2,1,0:T(4,128)S(1)} %fusion.33), channel_id=1, source_target_pairs={{16,0},{32,16},{48,32},{64,48},{80,64},{96,80},{112,96},{128,112},... | collective-permute-start | bytes 49160 | tf_op jit(solution)/shard_map/ppermute | solution.py:34
  (2 other events, 14.6 us)
